TPU v7x, 512 devices: a whole 4x8x8 slice. The times are simulated.
512 devices in a mesh: pair: 32 (over z_hi, x, core), row: 16 (over y, z_lo).
Axes of the slice: x: 4, y: 8, z: 8 (z_hi: 4, z_lo: 2; z = z_hi * 2 + z_lo), core: 2. Of those that a mesh axis runs over, the one named last changes fastest.
Arguments:
- matrix: bfloat16 [16384, 16384], P('row', 'pair'), may hold values from -60 to 60, as said below
Outputs:
- rotated: bfloat16 [16384, 16384], P('row', 'pair')
Inputs may be any that keep to these rules, and one draw needn't show every extreme that they name: `matrix`: symmetric; the block where a slot of even index meets another slot of even index, or odd meets odd, is zero.
All inputs are finite; a program needn't handle non-finite values.
Results may differ from a plain program's by a relative error of at most 0.012.
Values may be sent and summed in bfloat16 or wider, within the bound.
A program may use at most 128 MiB of HBM per device.

v0:
```python
import jax
import jax.numpy as jnp
from jax import lax
from jax.sharding import PartitionSpec as P

NS_ITERS = 3
ROUNDS = 2


epsilon = 1e-06


def cut_along(x, dim, size):
    lengths = x.shape
    tiles = x.reshape(*lengths[:dim], size, lengths[dim] // size, *lengths[dim + 1 :])
    return jnp.moveaxis(tiles, dim, 0)


def sent_and_summed(x, axis, dim):
    size = lax.axis_size(axis)
    tiles = lax.all_to_all(cut_along(x, dim, size), axis, 0, 0, tiled=True)
    return jnp.sum(tiles.astype(jnp.float32), axis=0)


def filled_up(lines, size):
    spare = -len(lines) % size
    return jnp.pad(lines, [(0, spare)] + [(0, 0)] * (lines.ndim - 1))


def joined_along(tiles, dim):
    lengths = list(tiles.shape[1:])
    lengths[dim] *= tiles.shape[0]
    return jnp.moveaxis(tiles, 0, dim).reshape(lengths)


def copy_for_each(x, axis):
    size = lax.axis_size(axis)
    return lax.all_to_all(jnp.broadcast_to(x[None], (size, *x.shape)), axis, 0, 0, tiled=True)


def gathered_copies(x, axis, dim):
    return joined_along(copy_for_each(x, axis), dim)


def sum_by_parts(x, axes):
    lines = x.reshape(-1)
    own = sent_and_summed(filled_up(lines, lax.axis_size(axes)), axes, 0)
    whole = gathered_copies(own.astype(jnp.bfloat16), axes, 0)
    return whole[: len(lines)].reshape(x.shape).astype(jnp.float32)


def broadcast(x, axis, root):
    return lax.dynamic_index_in_dim(lax.all_gather(x, axis), root, 0, keepdims=False)


def from_behind(x, axis, by):
    size = lax.axis_size(axis)
    pairs = [(i, i + by) for i in range(size) if 0 <= i + by < size]
    return lax.ppermute(x, axis, pairs)


def centered_start(pair_block):
    extent = pair_block.shape[0]
    identity = jnp.eye(extent, dtype=jnp.float32)
    offset = jnp.trace(pair_block) / extent
    centered = pair_block - offset * identity
    norm_value = jnp.sqrt(jnp.sum(centered * centered) + epsilon)
    return (centered / norm_value).astype(jnp.bfloat16)


def newton_rows(rows_iter, iterate):
    square = jnp.dot(rows_iter, iterate, preferred_element_type=jnp.float32).astype(jnp.bfloat16)
    cubic = jnp.dot(square, iterate, preferred_element_type=jnp.float32)
    return (1.5 * rows_iter.astype(jnp.float32) - 0.5 * cubic).astype(jnp.bfloat16)


def orthogonal_basis(iterate):
    extent = iterate.shape[0]
    middle = extent // 2
    sign_flip = jnp.concatenate(
        [jnp.ones((middle,), jnp.float32), -jnp.ones((middle,), jnp.float32)]
    )
    identity = jnp.eye(extent, dtype=jnp.float32)
    flipped = iterate.astype(jnp.float32) * sign_flip[None, :]
    spanning = 0.5 * (identity + flipped)
    inner_gram = lax.dot_general(
        iterate, iterate, (((0,), (0,)), ((), ())), preferred_element_type=jnp.float32
    )
    gram_matrix = 0.25 * (
        identity + flipped + flipped.T + sign_flip[:, None] * inner_gram * sign_flip[None, :]
    )
    factor = jnp.linalg.cholesky(gram_matrix)
    rotation = lax.linalg.triangular_solve(
        factor, spanning, left_side=False, lower=True, transpose_a=True
    )
    return rotation.astype(jnp.bfloat16)


def jacobi_round(current, row_index, pair_index):
    extent = current.shape[1]
    row_slab = lax.dynamic_slice_in_dim(current, pair_index % 2 * extent, extent, 0)
    holder = pair_index // 2 == row_index
    contribution = jnp.where(holder, row_slab.astype(jnp.float32), 0.0)
    pair_block = sum_by_parts(contribution.astype(jnp.bfloat16), "row")
    iterate = centered_start(pair_block)
    for repeat in range(NS_ITERS):
        iterate = newton_rows(iterate, iterate)
    rotation = orthogonal_basis(iterate)
    columns = jnp.dot(current, rotation, preferred_element_type=jnp.float32).astype(jnp.bfloat16)
    pieces = []
    for member in range(2):
        partner = broadcast(rotation, "pair", 2 * row_index + member)
        column_rows = columns[member * extent : (member + 1) * extent]
        product = lax.dot_general(
            partner, column_rows, (((0,), (0,)), ((), ())), preferred_element_type=jnp.float32
        )
        pieces.append(product.astype(jnp.bfloat16))
    return jnp.concatenate(pieces, 0)


def tournament_move(current, row_index, pair_index, row_total, pair_total):
    middle = current.shape[1] // 2
    slot_zero = current[:middle]
    slot_one = current[middle : 2 * middle]
    slot_two = current[2 * middle : 3 * middle]
    slot_three = current[3 * middle :]
    from_above = from_behind(slot_two, "row", 1)
    from_after = from_behind(slot_one, "row", -1)
    is_first = row_index == 0
    is_last = row_index == row_total - 1
    next_zero = jnp.where(is_first, slot_zero, from_above)
    next_two = jnp.where(is_first, slot_one, slot_zero)
    next_three = jnp.where(is_last, slot_two, from_after)
    moved_rows = jnp.concatenate([next_zero, slot_three, next_two, next_three], 0)
    top_slot = moved_rows[:, :middle]
    bottom = moved_rows[:, middle:]
    outgoing = jnp.where(pair_index == 0, bottom, top_slot)
    from_before = from_behind(outgoing, "pair", 1)
    from_next = from_behind(bottom, "pair", -1)
    new_top = jnp.where(pair_index == 0, top_slot, from_before)
    new_bottom = jnp.where(pair_index == pair_total - 1, top_slot, from_next)
    return jnp.concatenate([new_top, new_bottom], 1)


def local(matrix):
    row_index = lax.axis_index("row")
    pair_index = lax.axis_index("pair")
    row_total = lax.axis_size("row")
    pair_total = lax.axis_size("pair")
    current = matrix
    for round_number in range(ROUNDS):
        if round_number > 0:
            current = tournament_move(current, row_index, pair_index, row_total, pair_total)
        current = jacobi_round(current, row_index, pair_index)
    return current


def solution(mesh):
    in_specs = (P("row", "pair"),)
    out_specs = P("row", "pair")
    return jax.shard_map(local, mesh=mesh, in_specs=in_specs, out_specs=out_specs, check_vma=False)
```

profile of v0, /device:TPU:1, one launch (start us, length us, event | category | flops | bytes accessed | tf_op | source)
XLA Modules:
  0.0 792.1 jit_solution(10194968223169139645)
XLA Ops:
  12.7 25.1 %all_to_all.32 = bf16[16,2,8192]{2,1,0:T(2,128)(2,1)S(1)} all-to-all(bf16[16,2,8192]{2,1,0:T(2,128)(2,1)S(1)} %reshape.236), channel_id=1, replica_groups=mesh['pair'=32,'row'=16] {'row'}, dimensions={0} | all-to-all | bytes 1048576 | tf_op jit(solution)/shard_map/all_to_all | solution.py:21
  45.1 4.8 all-to-all-start.1
  53.0 11.8 %all-to-all-done.1 = bf16[16,2,8192]{2,1,0:T(2,128)(2,1)} async-done(((bf16[16,2,8192]{2,1,0:T(2,128)(2,1)}), bf16[16,2,8192]{2,1,0:T(2,128)(2,1)}, u32[]{:S(2)}, u32[]{:S(2)}) %all-to-all-start.1) | async-done | bytes 524320 | tf_op jit(solution)/shard_map/all_to_all | solution.py:38
  68.4 3.9 convert_reduce_fusion
  85.7 12.1 %cholesky.286 = f32[128,128]{1,0:T(8,128)S(1)} custom-call(f32[128,128]{1,0:T(8,128)S(1)} %cholesky.426), custom_call_target="Cholesky" | custom-call | tf_op jit(solution)/shard_map/jit(cholesky)/cholesky | solution.py:92
  98.0 9.8 %custom-call.27 = f32[1,128,128]{1,2,0:T(8,128)S(1)} custom-call(f32[1,128,128]{2,1,0:T(8,128)S(1)} %get-tuple-element.79), custom_call_target="InvertDiagBlocksLowerTriangular" | custom-call | tf_op jit(solution)/shard_map/jit(cholesky)/cholesky | solution.py:92
  110.3 11.7 %cholesky.305 = f32[128,128]{1,0:T(8,128)S(1)} custom-call(f32[128,128]{1,0:T(8,128)S(1)} %cholesky.430), custom_call_target="Cholesky" | custom-call | tf_op jit(solution)/shard_map/jit(cholesky)/cholesky | solution.py:92
  122.1 9.8 %custom-call.28 = f32[1,128,128]{1,2,0:T(8,128)S(1)} custom-call(f32[1,128,128]{2,1,0:T(8,128)S(1)} %get-tuple-element.76), custom_call_target="InvertDiagBlocksLowerTriangular" | custom-call | tf_op jit(solution)/shard_map/jit(cholesky)/cholesky | solution.py:92
  133.4 11.9 %cholesky.326 = f32[128,128]{1,0:T(8,128)S(1)} custom-call(f32[128,128]{1,0:T(8,128)S(1)} %cholesky.435), custom_call_target="Cholesky" | custom-call | tf_op jit(solution)/shard_map/jit(cholesky)/cholesky | solution.py:92
  146.1 9.8 %custom-call.29 = f32[1,128,128]{1,2,0:T(8,128)S(1)} custom-call(f32[1,128,128]{2,1,0:T(8,128)S(1)} %get-tuple-element.73), custom_call_target="InvertDiagBlocksLowerTriangular" | custom-call | tf_op jit(solution)/shard_map/jit(cholesky)/cholesky | solution.py:92
  157.3 11.7 %cholesky.343 = f32[128,128]{1,0:T(8,128)S(1)} custom-call(f32[128,128]{1,0:T(8,128)S(1)} %convolution_subtract_fusion.11), custom_call_target="Cholesky" | custom-call | tf_op jit(solution)/shard_map/jit(cholesky)/cholesky | solution.py:92
  173.1 8.5 %while.4 = (s32[]{:T(128)}, f32[512,512]{1,0:T(8,128)S(1)}, s32[4,2]{0,1:T(2,128)S(1)}, f32[4,128,128]{2,1,0:T(8,128)S(1)}, s32[]{:T(128)}) while((s32[]{:T(128)}, f32[512,512]{1,0:T(8,128)S(1)}, s32[4,2]{0,1:T(2,128)S(1)}, f32[4,128,128]{2,1,0:T(8,128)S(1)}, s32[]{:T(128)}) %tuple.62), condition=%wide.while_cond, body=%wide.while_body.sunk | while | flops 2 | bytes 131181 | solution.py:93
  181.6 39.7 %custom-call.30 = f32[4,128,128]{1,2,0:T(8,128)S(1)} custom-call(f32[4,128,128]{2,1,0:T(8,128)S(1)} %get-tuple-element.21), custom_call_target="InvertDiagBlocksLowerTriangular" | custom-call | tf_op jit(solution)/shard_map/triangular_solve/custom-call.3 | solution.py:93
  227.2 135.2 %all-gather.5.cloned.1.call-done = bf16[16384,512]{0,1:T(8,128)(2,1)} async-done(((bf16[512,512]{0,1:T(8,128)(2,1)}), bf16[16384,512]{0,1:T(8,128)(2,1)}) %all-gather.5.cloned.1.call-update) | async-done | bytes 16777232 | tf_op jit(solution)/shard_map/all_gather | solution.py:53
  362.4 22.5 %copy.59 = bf16[16384,512]{1,0:T(8,128)(2,1)} copy(bf16[16384,512]{0,1:T(8,128)(2,1)} %all-gather.5.cloned.1.call-done) | data formatting | bytes 33554432 | tf_op jit(solution)/shard_map/all_gather | solution.py:53
  395.0 8.8 %collective-permute-done.1 = bf16[256,512]{1,0:T(8,128)(2,1)S(1)} collective-permute-done((bf16[256,512]{1,0:T(8,128)(2,1)S(1)}, bf16[256,512]{1,0:T(8,128)(2,1)S(1)}, u32[]{:S(2)}, u32[]{:S(2)}) %collective-permute-start.1) | collective-permute-done | bytes 262176 | tf_op jit(solution)/shard_map/ppermute | solution.py:59
  404.0 4.7 collective-permute-start.2
  410.6 4.2 collective-permute-done.2
  414.8 4.4 collective-permute-done.3
  423.9 21.7 %all_to_all.33 = bf16[16,2,8192]{2,1,0:T(2,128)(2,1)S(1)} all-to-all(bf16[16,2,8192]{2,1,0:T(2,128)(2,1)S(1)} %reshape.240), channel_id=1, replica_groups=mesh['pair'=32,'row'=16] {'row'}, dimensions={0} | all-to-all | bytes 1048576 | tf_op jit(solution)/shard_map/all_to_all | solution.py:21
  457.0 12.2 %all-to-all-done.3 = bf16[16,2,8192]{2,1,0:T(2,128)(2,1)S(1)} async-done(((bf16[16,2,8192]{2,1,0:T(2,128)(2,1)}), bf16[16,2,8192]{2,1,0:T(2,128)(2,1)S(1)}, u32[]{:S(2)}, u32[]{:S(2)}) %all-to-all-start.3) | async-done | bytes 524320 | tf_op jit(solution)/shard_map/all_to_all | solution.py:38
  481.5 11.7 %cholesky.358 = f32[128,128]{1,0:T(8,128)S(1)} custom-call(f32[128,128]{1,0:T(8,128)S(1)} %cholesky.439), custom_call_target="Cholesky" | custom-call | tf_op jit(solution)/shard_map/jit(cholesky)/cholesky | solution.py:92
  493.4 9.8 %custom-call.31 = f32[1,128,128]{1,2,0:T(8,128)S(1)} custom-call(f32[1,128,128]{2,1,0:T(8,128)S(1)} %get-tuple-element.69), custom_call_target="InvertDiagBlocksLowerTriangular" | custom-call | tf_op jit(solution)/shard_map/jit(cholesky)/cholesky | solution.py:92
  503.9 12.1 %cholesky.377 = f32[128,128]{1,0:T(8,128)S(1)} custom-call(f32[128,128]{1,0:T(8,128)S(1)} %cholesky.443), custom_call_target="Cholesky" | custom-call | tf_op jit(solution)/shard_map/jit(cholesky)/cholesky | solution.py:92
  517.4 9.8 %custom-call.32 = f32[1,128,128]{1,2,0:T(8,128)S(1)} custom-call(f32[1,128,128]{2,1,0:T(8,128)S(1)} %get-tuple-element.66), custom_call_target="InvertDiagBlocksLowerTriangular" | custom-call | tf_op jit(solution)/shard_map/jit(cholesky)/cholesky | solution.py:92
  527.9 11.7 %cholesky.398 = f32[128,128]{1,0:T(8,128)S(1)} custom-call(f32[128,128]{1,0:T(8,128)S(1)} %cholesky.448), custom_call_target="Cholesky" | custom-call | tf_op jit(solution)/shard_map/jit(cholesky)/cholesky | solution.py:92
  540.3 9.8 %custom-call.33 = f32[1,128,128]{1,2,0:T(8,128)S(1)} custom-call(f32[1,128,128]{2,1,0:T(8,128)S(1)} %get-tuple-element.63), custom_call_target="InvertDiagBlocksLowerTriangular" | custom-call | tf_op jit(solution)/shard_map/jit(cholesky)/cholesky | solution.py:92
  550.9 11.7 %cholesky.415 = f32[128,128]{1,0:T(8,128)S(1)} custom-call(f32[128,128]{1,0:T(8,128)S(1)} %convolution_subtract_fusion.10), custom_call_target="Cholesky" | custom-call | tf_op jit(solution)/shard_map/jit(cholesky)/cholesky | solution.py:92
  566.0 8.1 %while.5 = (s32[]{:T(128)}, f32[512,512]{1,0:T(8,128)S(1)}, s32[4,2]{0,1:T(2,128)S(1)}, f32[4,128,128]{2,1,0:T(8,128)S(1)}, s32[]{:T(128)}) while((s32[]{:T(128)}, f32[512,512]{1,0:T(8,128)S(1)}, s32[4,2]{0,1:T(2,128)S(1)}, f32[4,128,128]{2,1,0:T(8,128)S(1)}, s32[]{:T(128)}) %tuple.72), condition=%wide.while_cond.clone, body=%wide.while_body.clone.sunk | while | flops 2 | bytes 131181 | solution.py:93
  574.1 39.3 %custom-call.34 = f32[4,128,128]{1,2,0:T(8,128)S(1)} custom-call(f32[4,128,128]{2,1,0:T(8,128)S(1)} %get-tuple-element.22), custom_call_target="InvertDiagBlocksLowerTriangular" | custom-call | tf_op jit(solution)/shard_map/triangular_solve/custom-call.3 | solution.py:93
  620.9 137.6 %all-gather.7.cloned.1.call-done = bf16[16384,512]{0,1:T(8,128)(2,1)} async-done(((bf16[512,512]{0,1:T(8,128)(2,1)}), bf16[16384,512]{0,1:T(8,128)(2,1)}) %all-gather.7.cloned.1.call-update) | async-done | bytes 16777232 | tf_op jit(solution)/shard_map/all_gather | solution.py:53
  758.5 22.5 %copy.60 = bf16[16384,512]{1,0:T(8,128)(2,1)} copy(bf16[16384,512]{0,1:T(8,128)(2,1)} %all-gather.7.cloned.1.call-done) | data formatting | bytes 33554432 | tf_op jit(solution)/shard_map/all_gather | solution.py:53
  (184 shorter events, 117.8 us)
Async XLA Ops:
  45.1 19.8 %all-to-all-start.1 = ((bf16[16,2,8192]{2,1,0:T(2,128)(2,1)}), bf16[16,2,8192]{2,1,0:T(2,128)(2,1)}, u32[]{:S(2)}, u32[]{:S(2)}) async-start(bf16[16,2,8192]{2,1,0:T(2,128)(2,1)} %reshape.238), calls=%async_computation.1 | async-start | bytes 1048576 | tf_op jit(solution)/shard_map/all_to_all | solution.py:38
  49.8 312.5 %all-gather.5.cloned.1.call-start = ((), (), s32[]{:S(2)}) async-start(), calls=%async_computation.4 | async-start | bytes 17301504 | tf_op jit(solution)/shard_map/all_gather | solution.py:53
  67.3 5.0 copy-start.2
  74.3 3.6 copy-start.1
  79.9 0.7 copy-start.10
  82.5 1.0 copy-start.11
  84.7 1.0 copy-start.3
  224.1 1.3 copy-start.9
  386.4 7.3 collective-permute-start
  393.7 10.1 %collective-permute-start.1 = (bf16[256,512]{1,0:T(8,128)(2,1)S(1)}, bf16[256,512]{1,0:T(8,128)(2,1)S(1)}, u32[]{:S(2)}, u32[]{:S(2)}) collective-permute-start(bf16[256,512]{1,0:T(8,128)(2,1)S(1)} %get-tuple-element.56), channel_id=1, source_target_pairs={{1,0},{2,1},{3,2},{4,3},{5,4},{6,5},{7,6},{8,7},{9,8},{10,9},{11,1... | collective-permute-start | bytes 786440 | tf_op jit(solution)/shard_map/ppermute | solution.py:59
  404.0 10.8 %collective-permute-start.2 = (bf16[1024,256]{1,0:T(8,128)(2,1)S(1)}, bf16[1024,256]{1,0:T(8,128)(2,1)S(1)}, u32[]{:S(2)}, u32[]{:S(2)}) collective-permute-start(bf16[1024,256]{1,0:T(8,128)(2,1)S(1)} %get-tuple-element.54), channel_id=1, source_target_pairs={{0,16},{16,32},{32,48},{48,64},{64,80},{80,96},{96,112},{112,128},... | collective-permute-start | bytes 1572872 | tf_op jit(solution)/shard_map/ppermute | solution.py:59
  408.7 10.5 %collective-permute-start.3 = (bf16[1024,256]{1,0:T(8,128)(2,1)S(1)}, bf16[1024,256]{1,0:T(8,128)(2,1)S(1)}, u32[]{:S(2)}, u32[]{:S(2)}) collective-permute-start(bf16[1024,256]{1,0:T(8,128)(2,1)S(1)} %get-tuple-element.53), channel_id=1, source_target_pairs={{16,0},{32,16},{48,32},{64,48},{80,64},{96,80},{112,96},{128,112},... | collective-permute-start | bytes 1572872 | tf_op jit(solution)/shard_map/ppermute | solution.py:59
  419.3 4.2 copy-start.4
  419.3 4.2 copy-start.6
  453.0 16.3 %all-to-all-start.3 = ((bf16[16,2,8192]{2,1,0:T(2,128)(2,1)}), bf16[16,2,8192]{2,1,0:T(2,128)(2,1)S(1)}, u32[]{:S(2)}, u32[]{:S(2)}) async-start(bf16[16,2,8192]{2,1,0:T(2,128)(2,1)} %reshape.242), calls=%async_computation.3 | async-start | bytes 1048576 | tf_op jit(solution)/shard_map/all_to_all | solution.py:38
  456.5 302.0 %all-gather.7.cloned.1.call-start = ((), (), s32[]{:S(2)}) async-start(), calls=%async_computation.5 | async-start | bytes 17301504 | tf_op jit(solution)/shard_map/all_gather | solution.py:53
  469.9 2.1 copy-start.8
  527.9 85.6 %copy-start = (f32[512,512]{1,0:T(8,128)S(1)}, f32[512,512]{1,0:T(8,128)}, u32[]{:S(2)}) copy-start(f32[512,512]{1,0:T(8,128)} %get-tuple-element.39) | copy-start | bytes 3145732
  616.3 2.8 copy-start.5
  616.3 2.8 copy-start.7
Sparse Core Ops, SparseCore 0:
  225.5 136.7 all-gather.4
  619.2 139.2 all-gather.6
where the time goes:
time: 803 us; the launch traced here: 792 us
  waiting for transfers between devices  318 us (40%)
  other arithmetic  271 us (34%)
  local copies, waits for them, and re-layouts  80.4 us (10%)
  blocking collectives  46.8 us (6%)
  matrix products  34.9 us (4%)
  between operations  22.3 us (3%)
  starting transfers between devices  18.2 us (2%)
    all_gather x2, waiting for transfers between devices, broadcast(): lax.all_gather(x, axis)  273 us
    another operation x29, other arithmetic, orthogonal_basis(): factor = jnp.linalg.cholesky(gram_matrix)  159 us
    another operation x5, other arithmetic, orthogonal_basis(): lax.linalg.triangular_solve(factor, spanning, left_side=False, lower=True...  79.3 us
    all_to_all x2, blocking collectives, sent_and_summed(): tiles = lax.all_to_all(cut_along(x, dim, size), axis, 0, 0, tiled=True)  46.8 us
    all_gather x2, local copies, waits for them, and re-layouts, broadcast(): lax.all_gather(x, axis)  44.9 us
    all_to_all x2, waiting for transfers between devices, copy_for_each(): lax.all_to_all(jnp.broadcast_to(x[None], (size, *x.shape)), axis, 0, 0, t...  24 us
    ppermute x4, waiting for transfers between devices, from_behind(): return lax.ppermute(x, axis, pairs)  21.2 us
    another operation x27, local copies, waits for them, and re-layouts, orthogonal_basis(): lax.linalg.triangular_solve(factor, spanning, left_side=False, lower=True...  16.5 us
  transfers between devices with their start and end apart: 8, of which 8 were waited for; matrix products, arithmetic and copies ran while one was open for 1% of the time, Pallas kernels for 0%

commit v1 on v0

v1 whole, which is shorter than its diff:
```python
import functools

import jax
import jax.numpy as jnp
from jax import lax
from jax.experimental import pallas as pl
from jax.experimental.pallas import tpu as pltpu
from jax.sharding import PartitionSpec as P

NS_ITERS = 3
EPS = 1e-06
F32 = jnp.float32
BF = jnp.bfloat16
HALT = 4e-4
WIDE = 0.9


def mm(a, b):
    return jnp.dot(a, b, preferred_element_type=F32)


def mm_nt(a, b):
    return lax.dot_general(a, b, (((1,), (1,)), ((), ())), preferred_element_type=F32)


def mm_tn(a, b):
    return lax.dot_general(a, b, (((0,), (0,)), ((), ())), preferred_element_type=F32)


def gather_kernel(nr, np_, a_ref, out_ref, buf, sc_sem, first_sem, ag_send, ag_recv, out_sem):
    r = lax.axis_index("row")
    q = lax.axis_index("pair")
    b = a_ref.shape[1] // 2
    s = b // nr

    def scatter(row0, col0, p, slot, sem):
        def body(i, carry):
            src = a_ref.at[
                pl.ds(pl.multiple_of(row0 + i * s, s), s), pl.ds(pl.multiple_of(col0, b), b)
            ]
            for chain in range(2):
                dr = i if chain == 0 else p // 2
                dq = p if chain == 0 else 2 * i + p % 2
                dst = buf.at[chain, i, slot]
                own = (dr == r) & (dq == q)

                @pl.when(jnp.logical_not(own))
                def _():
                    pltpu.make_async_remote_copy(
                        src_ref=src,
                        dst_ref=dst,
                        send_sem=sem,
                        recv_sem=first_sem.at[chain],
                        device_id={"pair": dq, "row": dr},
                        device_id_type=pl.DeviceIdType.MESH,
                    ).start()

                @pl.when(own)
                def _():
                    pltpu.make_async_copy(src, dst, first_sem.at[chain]).start()

            return carry

        lax.fori_loop(0, nr, body, 0)

    def drain(pieces, sem):
        ref = a_ref.at[pl.ds(0, pieces * s), pl.ds(0, b)]
        pltpu.make_async_copy(ref, ref, sem).wait()

    diag = q // 2 == r
    first, last = q == 0, q == np_ - 1
    edge = first | last
    away = (q >= 2) & (r == q // 2 - 1)
    tail = last & (r == nr - 1)
    off = away | ((q == 1) & (r == 0)) | tail

    @pl.when(diag)
    def _():
        base = (q % 2) * 2 * b
        f = first.astype(jnp.int32)
        scatter(
            base + f * b,
            (1 - f) * b,
            jnp.minimum(q + 1, np_ - 1),
            last.astype(jnp.int32),
            sc_sem.at[0],
        )
        scatter(
            base + (1 - f) * b, f * b, jnp.maximum(q - 1, 0), 1 - f, sc_sem.at[0]
        )

    @pl.when(off)
    def _():
        p = jnp.where(q == 1, 0, jnp.where(tail, np_ - 1, q - 1))
        base = jnp.where(away, q % 2, 0) * 2 * b
        scatter(base, b, p, 2, sc_sem.at[1])
        scatter(base + b, 0, p, 3, sc_sem.at[1])

    for chain in range(2):
        me = r if chain == 0 else q // 2
        own = buf.at[chain, me]
        pltpu.make_async_copy(own, own, first_sem.at[chain]).wait()

        def send(k, carry):
            peer = lax.rem(me + k, nr)
            pltpu.make_async_remote_copy(
                src_ref=own,
                dst_ref=own,
                send_sem=ag_send.at[chain],
                recv_sem=ag_recv.at[chain],
                device_id=(
                    {"pair": q, "row": peer}
                    if chain == 0
                    else {"pair": 2 * peer + q % 2, "row": r}
                ),
                device_id_type=pl.DeviceIdType.MESH,
            ).start()
            return carry

        lax.fori_loop(1, nr, send, 0)
    for chain in range(2):
        rest = buf.at[chain, pl.ds(0, nr - 1)]
        pltpu.make_async_copy(rest, rest, ag_recv.at[chain]).wait()
        pltpu.make_async_copy(buf.at[chain], out_ref.at[chain], out_sem.at[chain]).start()
    for chain in range(2):
        rest = buf.at[chain, pl.ds(0, nr - 1)]
        pltpu.make_async_copy(rest, rest, ag_send.at[chain]).wait()
        pltpu.make_async_copy(buf.at[chain], out_ref.at[chain], out_sem.at[chain]).wait()

    @pl.when(diag & edge)
    def _():
        drain(4 * nr - 2, sc_sem.at[0])

    @pl.when(diag & jnp.logical_not(edge))
    def _():
        drain(4 * nr, sc_sem.at[0])

    @pl.when(tail)
    def _():
        drain(4 * nr - 4, sc_sem.at[1])

    @pl.when(off & jnp.logical_not(tail))
    def _():
        drain(4 * nr, sc_sem.at[1])


def gathered(matrix, nr, np_):
    b = matrix.shape[1] // 2
    shape = (2, nr, 4, b // nr, b)
    return pl.pallas_call(
        functools.partial(gather_kernel, nr, np_),
        out_shape=jax.ShapeDtypeStruct(shape, BF),
        in_specs=[pl.BlockSpec(memory_space=pl.ANY)],
        out_specs=pl.BlockSpec(memory_space=pl.ANY),
        scratch_shapes=[
            pltpu.VMEM(shape, BF),
            pltpu.SemaphoreType.DMA((2,)),
            pltpu.SemaphoreType.DMA((2,)),
            pltpu.SemaphoreType.DMA((2,)),
            pltpu.SemaphoreType.DMA((2,)),
            pltpu.SemaphoreType.DMA((2,)),
        ],
        compiler_params=pltpu.CompilerParams(has_side_effects=True),
    )(matrix)


def upper_half(n):
    i = lax.broadcasted_iota(jnp.int32, (n, n), 0)
    j = lax.broadcasted_iota(jnp.int32, (n, n), 1)
    return jnp.where(i < j, 1.0, jnp.where(i == j, 0.5, 0.0)).astype(F32)


def unit(n):
    i = lax.broadcasted_iota(jnp.int32, (n, n), 0)
    j = lax.broadcasted_iota(jnp.int32, (n, n), 1)
    return jnp.where(i == j, 1.0, 0.0).astype(F32)


def direct_factor(d_ref, v_ref):
    n = d_ref.shape[0]
    lane = lax.broadcasted_iota(jnp.int32, (1, n), 1)
    line = lax.broadcasted_iota(jnp.int32, (n, 1), 0)
    v_ref[...] = unit(n)
    d_ref[...] += unit(n)

    def step(k, carry):
        row = d_ref[pl.ds(k, 1), :]
        made = v_ref[pl.ds(k, 1), :]
        pivot = jnp.sum(jnp.where(lane == k, row, 0.0), axis=1, keepdims=True)
        column = jnp.sum(jnp.where(lane == k, d_ref[...], 0.0), axis=1, keepdims=True)
        column = jnp.where(line > k, column, 0.0) / pivot
        d_ref[...] -= column * row
        v_ref[...] -= column * made
        v_ref[pl.ds(k, 1), :] = made * lax.rsqrt(pivot)
        return carry

    lax.fori_loop(0, n, step, 0)
    v_ref[...] = v_ref[...].T - unit(n)


def inverse_factor(d_ref, e_ref, v_ref):
    n = d_ref.shape[0]
    h = n // 2
    d = d_ref[...]
    e_ref[...] = d
    v_ref[...] = jnp.zeros((n, n), F32)
    largest = jnp.max(jnp.abs(d))

    def step(state):
        count, _ = state
        up = upper_half(n)
        d = e_ref[...]
        t32 = d * up
        low32 = d - t32
        t = t32.astype(BF)
        low = low32.astype(BF)
        db = d.astype(BF)
        v = v_ref[...].astype(BF)
        left = mm(db[:, :h], t[:h, :h])
        right = mm(db, t[:, h:])
        w = jnp.concatenate([left, right], 1)
        g = (low32 - w).astype(BF)
        z = jnp.concatenate([mm(low[:h, :h], g[:h]), mm(low[h:], g)], 0)
        new = -w - z
        e_ref[...] = new
        v_ref[:h, :h] += -t32[:h, :h] - mm(v[:h, :h], t[:h, :h])
        v_ref[:h, h:] += -t32[:h, h:] - mm(v[:h], t[:, h:])
        v_ref[h:, h:] += -t32[h:, h:] - mm(v[h:, h:], t[h:, h:])
        return count + 1, jnp.sum(new * new)

    def more(state):
        count, residual = state
        return (count < 10) & (residual > HALT) & (largest < WIDE)

    _, residual = lax.while_loop(more, step, (jnp.int32(0), jnp.float32(1.0)))

    @pl.when(jnp.logical_not((residual <= HALT) & (largest < WIDE)))
    def _():
        direct_factor(d_ref, v_ref)


def half_rotation(c, half, d_ref, e_ref, v_ref):
    b = c.shape[0]
    c32 = c.astype(F32)
    norm = jnp.sqrt(2.0 * jnp.sum(c32 * c32) + EPS)
    y = (c32 / norm).astype(BF)
    for _ in range(NS_ITERS):
        square = mm_nt(y, y).astype(BF)
        y = (1.5 * y.astype(F32) - 0.5 * mm(square, y)).astype(BF)
    d_ref[...] = mm_nt(y, y)
    inverse_factor(d_ref, e_ref, v_ref)
    v = v_ref[...]
    same = (unit(b) + v).astype(BF)
    yt = y.T
    other = yt.astype(F32) + mm(yt, v.astype(BF))
    other = jnp.where(half == 0, other, -other).astype(BF)
    return same, other


def chain_kernel(nr, np_, quad_ref, out_ref, d1, e1, v1, d2, e2, v2):
    r = lax.axis_index("row")
    q = lax.axis_index("pair")
    chain = pl.program_id(0)
    p = jnp.where(chain == 0, q, 2 * r + q % 2)
    half_a = (p == 1).astype(jnp.int32)
    half_b = (p != np_ - 1).astype(jnp.int32)
    b = quad_ref.shape[-1]
    ca, cb, cab, dab = [quad_ref[:, k].reshape(b, b) for k in range(4)]

    def diagonal(c, same, other):
        first = mm_tn(same, mm(c, other).astype(BF))
        second = mm_tn(other, mm_tn(c, same).astype(BF))
        return (first + second).astype(BF)

    same, other = half_rotation(ca, half_a, d1, e1, v1)
    aa = diagonal(ca, same, other)
    a_even = jnp.where(half_a == 0, same, other)
    a_odd = jnp.where(half_a == 0, other, same)
    out_ref[0:b, 0:b] = a_even
    out_ref[b : 2 * b, 0:b] = a_odd
    same, other = half_rotation(cb, half_b, d1, e1, v1)
    bb = diagonal(cb, same, other)
    b_even = jnp.where(half_b == 0, same, other)
    b_odd = jnp.where(half_b == 0, other, same)
    out_ref[0:b, b : 2 * b] = b_even
    out_ref[b : 2 * b, b : 2 * b] = b_odd
    upper = mm(cab, b_odd).astype(BF)
    lower = mm(dab, b_even).astype(BF)
    ab = (mm_tn(a_even, upper) + mm_tn(a_odd, lower)).astype(BF)
    ba = (mm_tn(upper, a_even) + mm_tn(lower, a_odd)).astype(BF)

    n = 2 * b
    block = jnp.concatenate(
        [jnp.concatenate([aa, ab], 1), jnp.concatenate([ba, bb], 1)], 0
    ).astype(F32)
    eye = unit(n)
    offset = jnp.sum(block * eye) / n
    block = block - offset * eye
    x = (block / jnp.sqrt(jnp.sum(block * block) + EPS)).astype(BF)
    for _ in range(NS_ITERS):
        square = mm(x, x).astype(BF)
        x = (1.5 * x.astype(F32) - 0.5 * mm(square, x)).astype(BF)
    inner = mm(x, x)
    x32 = x.astype(F32)
    d2[:b, :b] = inner[:b, :b] + 2.0 * x32[:b, :b]
    d2[:b, b:] = -inner[:b, b:]
    d2[b:, :b] = -inner[b:, :b]
    d2[b:, b:] = inner[b:, b:] - 2.0 * x32[b:, b:]
    inverse_factor(d2, e2, v2)
    flipped = jnp.concatenate([x[:, :b], -x[:, b:]], 1)
    v = v2[...]
    out_ref[2 * b :, :] = (eye + v + flipped.astype(F32) + mm(flipped, v.astype(BF))).astype(BF)


def chains(quads, nr, np_):
    b = quads.shape[-1]
    return pl.pallas_call(
        functools.partial(chain_kernel, nr, np_),
        grid=(2,),
        out_shape=jax.ShapeDtypeStruct((2, 4 * b, 2 * b), BF),
        in_specs=[pl.BlockSpec((None, *quads.shape[1:]), lambda c: (c, 0, 0, 0, 0))],
        out_specs=pl.BlockSpec((None, 4 * b, 2 * b), lambda c: (c, 0, 0)),
        scratch_shapes=[pltpu.VMEM((b, b), F32)] * 3 + [pltpu.VMEM((2 * b, 2 * b), F32)] * 3,
        compiler_params=pltpu.CompilerParams(dimension_semantics=("arbitrary",)),
        cost_estimate=pl.CostEstimate(
            flops=60 * (2 * b) ** 3, bytes_accessed=2 * 12 * b * b, transcendentals=0
        ),
    )(quads)


def update_kernel(left_ref, right_ref, col_ref, own_ref, other_ref, out_ref, mid):
    core = lax.axis_index("pair") % 2
    b = left_ref.shape[-1]
    for side, ref in enumerate((left_ref, right_ref)):
        cols = slice(side * b, (side + 1) * b)
        even = col_ref[0:b, cols]
        odd = col_ref[b : 2 * b, cols]
        for k in range(4):
            mid[k, :b, cols] = mm(ref[k, 0], odd).astype(BF)
            mid[k, b:, cols] = mm(ref[k, 1], even).astype(BF)
    turn = col_ref[2 * b :, :]
    for ref, local in ((own_ref, core), (other_ref, 1 - core)):
        top = mm_tn(ref[: 2 * b, :b], mid[local])
        bottom = mm_tn(ref[: 2 * b, b:], mid[local + 2])
        current = jnp.concatenate([top, bottom], 0).astype(BF)
        columns = mm(current, turn).astype(BF)
        out_ref[pl.ds(pl.multiple_of(local * 2 * b, 2 * b), 2 * b), :] = mm_tn(
            ref[2 * b :, :], columns
        ).astype(BF)


def updated(left, right, col, own, other):
    b = left.shape[-1]
    return pl.pallas_call(
        update_kernel,
        out_shape=jax.ShapeDtypeStruct((4 * b, 2 * b), BF),
        in_specs=[pl.BlockSpec(memory_space=pltpu.VMEM)] * 5,
        out_specs=pl.BlockSpec(memory_space=pltpu.VMEM),
        scratch_shapes=[pltpu.VMEM((4, 2 * b, 2 * b), BF)],
    )(left, right, col, own, other)


def from_behind(x, axis, by):
    size = lax.axis_size(axis)
    pairs = [(i, i + by) for i in range(size) if 0 <= i + by < size]
    return lax.ppermute(x, axis, pairs)


def local(matrix):
    r = lax.axis_index("row")
    q = lax.axis_index("pair")
    nr = lax.axis_size("row")
    np_ = lax.axis_size("pair")
    b = matrix.shape[1] // 2
    quads = gathered(matrix, nr, np_)
    matrix, quads = lax.optimization_barrier((matrix, quads))
    packed = jnp.stack(
        [
            jnp.stack([matrix[2 * k * b : (2 * k + 1) * b, b:], matrix[(2 * k + 1) * b : (2 * k + 2) * b, :b]])
            for k in range(2)
        ]
    )
    above = jnp.where(r == 0, packed[0], from_behind(packed[1], "row", 1))
    below = jnp.where(r == nr - 1, packed[1], from_behind(packed[0], "row", -1))
    ext = jnp.stack([above, packed[0], packed[1], below])
    left = jnp.where(q == 0, ext, from_behind(ext, "pair", 1))
    right = jnp.where(q == np_ - 1, ext, from_behind(ext, "pair", -1))
    turns = chains(quads, nr, np_)
    other = lax.ppermute(turns[1], "pair", [(i, i ^ 1) for i in range(np_)])
    return updated(left, right, turns[0], turns[1], other)


def solution(mesh):
    return jax.shard_map(
        local, mesh=mesh, in_specs=(P("row", "pair"),), out_specs=P("row", "pair"), check_vma=False
    )
```

time: 803 us -> 123 us (0.15)
  the two profiles are of different devices: /device:TPU:1 before, /device:TPU:63 now
where the time goes in v1:
time: 123 us
  Pallas kernels  88.1 us (72%)
  starting transfers between devices  14.3 us (12%)
  waiting for transfers between devices  14.3 us (12%)
  other arithmetic  3.37 us (3%)
  local copies, waits for them, and re-layouts  2.69 us (2%)
    pallas_call x1, Pallas kernels, gathered(): pl.pallas_call(functools.partial(gather_kernel, nr, np_), out_shape=jax.S...  53.4 us
    pallas_call x1, Pallas kernels, chains(): pl.pallas_call(functools.partial(chain_kernel, nr, np_), grid=(2,), out_s...  28.6 us
    ppermute x4, waiting for transfers between devices, from_behind(): return lax.ppermute(x, axis, pairs)  14.3 us
    ppermute x4, starting transfers between devices, from_behind(): return lax.ppermute(x, axis, pairs)  12.4 us
    pallas_call x1, Pallas kernels, updated(): pl.pallas_call(update_kernel, out_shape=jax.ShapeDtypeStruct((4 * b, 2 *...  6.11 us
    select_n x1, other arithmetic, local(): right = jnp.where(q == np_ - 1, ext, from_behind(ext, 'pair', -1))  3.11 us
    squeeze x1, local copies, waits for them, and re-layouts, local(): return updated(left, right, turns[0], turns[1], other)  2.64 us
  transfers between devices with their start and end apart: 5, of which 2 were waited for; matrix products, arithmetic and copies ran while one was open for 5% of the time, Pallas kernels for 23%

profile of v1, /device:TPU:63, one launch (start us, length us, event | category | flops | bytes accessed | tf_op | source)
XLA Modules:
  0.0 122.8 jit_solution(15568408382906531239)
XLA Ops:
  0.0 0.0 copy-start.1
  0.0 53.4 %shard_map.17.quad_ref = bf16[2,16,4,16,256]{4,3,2,1,0:T(8,128)(2,1)} custom-call(bf16[1024,512]{1,0:T(8,128)(2,1)} %a_ref.1), custom_call_target="tpu_custom_call" | custom-call | tf_op jit(solution)/shard_map/pallas_call | solution.py:150
  53.4 0.0 copy-done.1
  53.5 1.9 %collective-permute-start = (bf16[2,256,256]{2,1,0:T(8,128)(2,1)S(1)}, bf16[2,256,256]{2,1,0:T(8,128)(2,1)S(1)}, u32[]{:S(2)}, u32[]{:S(2)}) collective-permute-start(bf16[2,256,256]{2,1,0:T(8,128)(2,1)S(1)} %get-tuple-element.20), channel_id=1, source_target_pairs={{0,1},{1,2},{2,3},{3,4},{4,5},{5,6},{6,7},{7,8},{8,9},{9,10},{10,1... | collective-permute-start | bytes 786440 | tf_op jit(solution)/shard_map/ppermute | solution.py:366
  55.4 8.0 %collective-permute-done = bf16[2,256,256]{2,1,0:T(8,128)(2,1)S(1)} collective-permute-done((bf16[2,256,256]{2,1,0:T(8,128)(2,1)S(1)}, bf16[2,256,256]{2,1,0:T(8,128)(2,1)S(1)}, u32[]{:S(2)}, u32[]{:S(2)}) %collective-permute-start) | collective-permute-done | bytes 262176 | tf_op jit(solution)/shard_map/ppermute | solution.py:366
  63.4 0.1 select_bitcast_fusion.1
  63.5 1.9 %collective-permute-start.1 = (bf16[2,256,256]{2,1,0:T(8,128)(2,1)S(1)}, bf16[2,256,256]{2,1,0:T(8,128)(2,1)S(1)}, u32[]{:S(2)}, u32[]{:S(2)}) collective-permute-start(bf16[2,256,256]{2,1,0:T(8,128)(2,1)S(1)} %get-tuple-element.19), channel_id=1, source_target_pairs={{1,0},{2,1},{3,2},{4,3},{5,4},{6,5},{7,6},{8,7},{9,8},{10,9},{11,1... | collective-permute-start | bytes 786440 | tf_op jit(solution)/shard_map/ppermute | solution.py:366
  65.4 6.3 %collective-permute-done.1 = bf16[2,256,256]{2,1,0:T(8,128)(2,1)S(1)} collective-permute-done((bf16[2,256,256]{2,1,0:T(8,128)(2,1)S(1)}, bf16[2,256,256]{2,1,0:T(8,128)(2,1)S(1)}, u32[]{:S(2)}, u32[]{:S(2)}) %collective-permute-start.1) | collective-permute-done | bytes 262176 | tf_op jit(solution)/shard_map/ppermute | solution.py:366
  71.7 0.1 pad_maximum_fusion
  71.9 4.3 %collective-permute-start.3 = (bf16[4,2,256,256]{3,2,1,0:T(8,128)(2,1)S(1)}, bf16[4,2,256,256]{3,2,1,0:T(8,128)(2,1)}, u32[]{:S(2)}, u32[]{:S(2)}) collective-permute-start(bf16[4,2,256,256]{3,2,1,0:T(8,128)(2,1)S(1)} %pad_maximum_fusion), channel_id=1, source_target_pairs={{16,0},{32,16},{48,32},{64,48},{80,64},{96,80},{112,96},{128,112},... | collective-permute-start | bytes 3145736 | tf_op jit(solution)/shard_map/ppermute | solution.py:366
  76.2 4.2 %collective-permute-start.2 = (bf16[4,2,256,256]{3,2,1,0:T(8,128)(2,1)S(1)}, bf16[4,2,256,256]{3,2,1,0:T(8,128)(2,1)}, u32[]{:S(2)}, u32[]{:S(2)}) collective-permute-start(bf16[4,2,256,256]{3,2,1,0:T(8,128)(2,1)S(1)} %pad_maximum_fusion), channel_id=1, source_target_pairs={{0,16},{16,32},{32,48},{48,64},{64,80},{80,96},{96,112},{112,128},... | collective-permute-start | bytes 3145736 | tf_op jit(solution)/shard_map/ppermute | solution.py:366
  80.4 28.6 %shard_map.18 = bf16[2,1024,512]{2,1,0:T(8,128)(2,1)} custom-call(bf16[2,16,4,16,256]{4,3,2,1,0:T(8,128)(2,1)} %shard_map.17.quad_ref), custom_call_target="tpu_custom_call" | custom-call | flops 8053063680 | bytes 1572864 | tf_op jit(solution)/shard_map/pallas_call | solution.py:317
  109.0 2.6 %slice_bitcast_fusion = (bf16[1024,512]{1,0:T(8,128)(2,1)S(1)}, bf16[1024,512]{1,0:T(8,128)(2,1)}) fusion(bf16[2,1024,512]{2,1,0:T(8,128)(2,1)} %shard_map.18), kind=kLoop, calls=%fused_computation | loop fusion | bytes 4194304 | tf_op jit(solution)/shard_map/squeeze | solution.py:390
  111.7 0.0 copy-start
  111.7 1.9 %collective-permute-start.4 = (bf16[1024,512]{1,0:T(8,128)(2,1)S(1)}, bf16[1024,512]{1,0:T(8,128)(2,1)}, u32[]{:S(2)}, u32[]{:S(2)}) collective-permute-start(bf16[1024,512]{1,0:T(8,128)(2,1)S(1)} %get-tuple-element.9.own_ref), channel_id=1, source_target_pairs={{0,16},{16,0},{32,48},{48,32},{64,80},{80,64},{96,112},{112,96},{1... | collective-permute-start | bytes 3145736 | tf_op jit(solution)/shard_map/ppermute | solution.py:389
  113.6 0.0 collective-permute-done.3
  113.6 0.0 collective-permute-done.2
  113.6 3.1 %broadcast_select_fusion = (bf16[4,2,256,256]{3,2,1,0:T(8,128)(2,1)}, bf16[4,2,256,256]{3,2,1,0:T(8,128)(2,1)}) fusion(bf16[4,2,256,256]{3,2,1,0:T(8,128)(2,1)} %collective-permute-done.3, pred[]{:T(512)S(6)} %eq.15, bf16[1,2,256,256]{3,2,1,0:T(8,128)(2,1)S(1)} %select_bitcast_fusion, bf16[1,2,256,256]{3,2,1,0:T(8,128)(2,1)S(1)} %get-tuple-element.21, ...), kind=kLoop, calls=%fused_computation.3 | loop fusion | flops 2621440 | bytes 5242882 | tf_op jit(solution)/shard_map/jit(_where)/select_n | solution.py:387
  116.7 0.0 copy-done
  116.7 0.0 collective-permute-done.4.other_ref
  116.7 6.1 %shard_map.19 = bf16[1024,512]{1,0:T(8,128)(2,1)} custom-call(bf16[4,2,256,256]{3,2,1,0:T(8,128)(2,1)} %get-tuple-element.12.left_ref, bf16[4,2,256,256]{3,2,1,0:T(8,128)(2,1)} %get-tuple-element.11.right_ref, bf16[1024,512]{1,0:T(8,128)(2,1)} %get-tuple-element.10.col_ref, bf16[1024,512]{1,0:T(8,128)(2,1)} %copy-done, ...), custom_call_target="tpu_custom_call" | custom-call | tf_op jit(solution)/shard_map/pallas_call | solution.py:354
  (3 shorter events, 0.1 us)
Async XLA Ops:
  0.0 53.4 %copy-start.1 = (bf16[1024,512]{1,0:T(8,128)(2,1)S(1)}, bf16[1024,512]{1,0:T(8,128)(2,1)}, u32[]{:S(2)}) copy-start(bf16[1024,512]{1,0:T(8,128)(2,1)} %a_ref.1) | copy-start | bytes 3145732
  53.5 9.9 %collective-permute-start = (bf16[2,256,256]{2,1,0:T(8,128)(2,1)S(1)}, bf16[2,256,256]{2,1,0:T(8,128)(2,1)S(1)}, u32[]{:S(2)}, u32[]{:S(2)}) collective-permute-start(bf16[2,256,256]{2,1,0:T(8,128)(2,1)S(1)} %get-tuple-element.20), channel_id=1, source_target_pairs={{0,1},{1,2},{2,3},{3,4},{4,5},{5,6},{6,7},{7,8},{8,9},{9,10},{10,1... | collective-permute-start | bytes 786440 | tf_op jit(solution)/shard_map/ppermute | solution.py:366
  63.5 8.2 %collective-permute-start.1 = (bf16[2,256,256]{2,1,0:T(8,128)(2,1)S(1)}, bf16[2,256,256]{2,1,0:T(8,128)(2,1)S(1)}, u32[]{:S(2)}, u32[]{:S(2)}) collective-permute-start(bf16[2,256,256]{2,1,0:T(8,128)(2,1)S(1)} %get-tuple-element.19), channel_id=1, source_target_pairs={{1,0},{2,1},{3,2},{4,3},{5,4},{6,5},{7,6},{8,7},{9,8},{10,9},{11,1... | collective-permute-start | bytes 786440 | tf_op jit(solution)/shard_map/ppermute | solution.py:366
  71.9 41.7 %collective-permute-start.3 = (bf16[4,2,256,256]{3,2,1,0:T(8,128)(2,1)S(1)}, bf16[4,2,256,256]{3,2,1,0:T(8,128)(2,1)}, u32[]{:S(2)}, u32[]{:S(2)}) collective-permute-start(bf16[4,2,256,256]{3,2,1,0:T(8,128)(2,1)S(1)} %pad_maximum_fusion), channel_id=1, source_target_pairs={{16,0},{32,16},{48,32},{64,48},{80,64},{96,80},{112,96},{128,112},... | collective-permute-start | bytes 3145736 | tf_op jit(solution)/shard_map/ppermute | solution.py:366
  76.2 37.4 %collective-permute-start.2 = (bf16[4,2,256,256]{3,2,1,0:T(8,128)(2,1)S(1)}, bf16[4,2,256,256]{3,2,1,0:T(8,128)(2,1)}, u32[]{:S(2)}, u32[]{:S(2)}) collective-permute-start(bf16[4,2,256,256]{3,2,1,0:T(8,128)(2,1)S(1)} %pad_maximum_fusion), channel_id=1, source_target_pairs={{0,16},{16,32},{32,48},{48,64},{64,80},{80,96},{96,112},{112,128},... | collective-permute-start | bytes 3145736 | tf_op jit(solution)/shard_map/ppermute | solution.py:366
  111.7 5.1 %copy-start = (bf16[1024,512]{1,0:T(8,128)(2,1)}, bf16[1024,512]{1,0:T(8,128)(2,1)S(1)}, u32[]{:S(2)}) copy-start(bf16[1024,512]{1,0:T(8,128)(2,1)S(1)} %get-tuple-element.9.own_ref) | copy-start | bytes 3145732
  111.7 5.1 %collective-permute-start.4 = (bf16[1024,512]{1,0:T(8,128)(2,1)S(1)}, bf16[1024,512]{1,0:T(8,128)(2,1)}, u32[]{:S(2)}, u32[]{:S(2)}) collective-permute-start(bf16[1024,512]{1,0:T(8,128)(2,1)S(1)} %get-tuple-element.9.own_ref), channel_id=1, source_target_pairs={{0,16},{16,0},{32,48},{48,32},{64,80},{80,64},{96,112},{112,96},{1... | collective-permute-start | bytes 3145736 | tf_op jit(solution)/shard_map/ppermute | solution.py:389

commit v2 on v0

v2 whole, which is shorter than its diff:
```python
import functools

import jax
import jax.numpy as jnp
from jax import lax
from jax.experimental import pallas as pl
from jax.experimental.pallas import tpu as pltpu
from jax.sharding import PartitionSpec as P

NS_ITERS = 3
EPS = 1e-06
F32 = jnp.float32
BF = jnp.bfloat16
HALT = 4e-4
WIDE = 0.9


def mm(a, b):
    return jnp.dot(a, b, preferred_element_type=F32)


def mm_nt(a, b):
    return lax.dot_general(a, b, (((1,), (1,)), ((), ())), preferred_element_type=F32)


def mm_tn(a, b):
    return lax.dot_general(a, b, (((0,), (0,)), ((), ())), preferred_element_type=F32)


def upper_half(n):
    i = lax.broadcasted_iota(jnp.int32, (n, n), 0)
    j = lax.broadcasted_iota(jnp.int32, (n, n), 1)
    return jnp.where(i < j, 1.0, jnp.where(i == j, 0.5, 0.0)).astype(F32)


def unit(n):
    i = lax.broadcasted_iota(jnp.int32, (n, n), 0)
    j = lax.broadcasted_iota(jnp.int32, (n, n), 1)
    return jnp.where(i == j, 1.0, 0.0).astype(F32)


def direct_factor(d_ref, v_ref):
    n = d_ref.shape[0]
    lane = lax.broadcasted_iota(jnp.int32, (1, n), 1)
    line = lax.broadcasted_iota(jnp.int32, (n, 1), 0)
    v_ref[...] = unit(n)
    d_ref[...] += unit(n)

    def step(k, carry):
        row = d_ref[pl.ds(k, 1), :]
        made = v_ref[pl.ds(k, 1), :]
        pivot = jnp.sum(jnp.where(lane == k, row, 0.0), axis=1, keepdims=True)
        column = jnp.sum(jnp.where(lane == k, d_ref[...], 0.0), axis=1, keepdims=True)
        column = jnp.where(line > k, column, 0.0) / pivot
        d_ref[...] -= column * row
        v_ref[...] -= column * made
        v_ref[pl.ds(k, 1), :] = made * lax.rsqrt(pivot)
        return carry

    lax.fori_loop(0, n, step, 0)
    v_ref[...] = v_ref[...].T - unit(n)


def factor_step(d, v):
    n = d.shape[0]
    h = n // 2
    t32 = d * upper_half(n)
    low32 = d - t32
    t = t32.astype(BF)
    low = low32.astype(BF)
    db = d.astype(BF)
    w = jnp.concatenate([mm(db[:, :h], t[:h, :h]), mm(db, t[:, h:])], 1)
    g = (low32 - w).astype(BF)
    new = -w - jnp.concatenate([mm(low[:h, :h], g[:h]), mm(low[h:], g)], 0)
    if v is None:
        return new, -t32
    vb = v.astype(BF)
    top = jnp.concatenate([mm(vb[:h, :h], t[:h, :h]), mm(vb[:h], t[:, h:])], 1)
    bottom = jnp.concatenate([jnp.zeros((n - h, h), F32), mm(vb[h:, h:], t[h:, h:])], 1)
    return new, v - t32 - jnp.concatenate([top, bottom], 0)


def steps_factor(steps):
    def factor(d):
        largest = jnp.max(jnp.abs(d))
        v = None
        for _ in range(steps[d.shape[0]]):
            d, v = factor_step(d, v)
        return v, jnp.sum(d * d), largest

    return factor


def full_factor(refs):
    def factor(d):
        d_ref, e_ref, v_ref = refs[d.shape[0]]
        d_ref[...] = d
        e_ref[...] = d
        v_ref[...] = jnp.zeros(d.shape, F32)
        largest = jnp.max(jnp.abs(d))

        def step(state):
            new, v = factor_step(e_ref[...], v_ref[...])
            e_ref[...] = new
            v_ref[...] = v
            return state[0] + 1, jnp.sum(new * new)

        def more(state):
            return (state[0] < 10) & (state[1] > HALT) & (largest < WIDE)

        _, residual = lax.while_loop(more, step, (jnp.int32(0), jnp.float32(1.0)))

        @pl.when(jnp.logical_not((residual <= HALT) & (largest < WIDE)))
        def _():
            direct_factor(d_ref, v_ref)

        return v_ref[...], residual, largest

    return factor


def half_rotation(c, half, factor):
    b = c.shape[0]
    c32 = c.astype(F32)
    norm = jnp.sqrt(2.0 * jnp.sum(c32 * c32) + EPS)
    y = (c32 / norm).astype(BF)
    for _ in range(NS_ITERS):
        square = mm_nt(y, y).astype(BF)
        y = (1.5 * y.astype(F32) - 0.5 * mm(square, y)).astype(BF)
    v, residual, largest = factor(mm_nt(y, y))
    same = (unit(b) + v).astype(BF)
    yt = y.T
    other = yt.astype(F32) + mm(yt, v.astype(BF))
    other = jnp.where(half == 0, other, -other).astype(BF)
    return same, other, (residual, largest)


def rotations(blocks, p, np_, out_ref, factor):
    half_a = (p == 1).astype(jnp.int32)
    half_b = (p != np_ - 1).astype(jnp.int32)
    ca, cb, cab, dab = blocks
    b = ca.shape[0]

    def diagonal(c, same, other):
        first = mm_tn(same, mm(c, other).astype(BF))
        second = mm_tn(other, mm_tn(c, same).astype(BF))
        return (first + second).astype(BF)

    same, other, fit_a = half_rotation(ca, half_a, factor)
    aa = diagonal(ca, same, other)
    a_even = jnp.where(half_a == 0, same, other)
    a_odd = jnp.where(half_a == 0, other, same)
    out_ref[0:b, 0:b] = a_even
    out_ref[b : 2 * b, 0:b] = a_odd
    same, other, fit_b = half_rotation(cb, half_b, factor)
    bb = diagonal(cb, same, other)
    b_even = jnp.where(half_b == 0, same, other)
    b_odd = jnp.where(half_b == 0, other, same)
    out_ref[0:b, b : 2 * b] = b_even
    out_ref[b : 2 * b, b : 2 * b] = b_odd
    upper = mm(cab, b_odd).astype(BF)
    lower = mm(dab, b_even).astype(BF)
    ab = (mm_tn(a_even, upper) + mm_tn(a_odd, lower)).astype(BF)
    ba = (mm_tn(upper, a_even) + mm_tn(lower, a_odd)).astype(BF)

    n = 2 * b
    block = jnp.concatenate(
        [jnp.concatenate([aa, ab], 1), jnp.concatenate([ba, bb], 1)], 0
    ).astype(F32)
    eye = unit(n)
    offset = jnp.sum(block * eye) / n
    block = block - offset * eye
    x = (block / jnp.sqrt(jnp.sum(block * block) + EPS)).astype(BF)
    for _ in range(NS_ITERS):
        square = mm(x, x).astype(BF)
        x = (1.5 * x.astype(F32) - 0.5 * mm(square, x)).astype(BF)
    inner = mm(x, x)
    x32 = x.astype(F32)
    d = jnp.concatenate(
        [
            jnp.concatenate([inner[:b, :b] + 2.0 * x32[:b, :b], -inner[:b, b:]], 1),
            jnp.concatenate([-inner[b:, :b], inner[b:, b:] - 2.0 * x32[b:, b:]], 1),
        ],
        0,
    )
    v, residual, largest = factor(d)
    flipped = jnp.concatenate([x[:, :b], -x[:, b:]], 1)
    out_ref[2 * b :, :] = (eye + v + flipped.astype(F32) + mm(flipped, v.astype(BF))).astype(BF)
    return (*fit_a, *fit_b, residual, largest)


def turn_kernel(
    nr, np_, a_ref, turns_out, tiles_out, quads_out, fits_out,
    buf, turns, tiles, ext, fits, sc_sem, first_sem, ag_send, ag_recv,
    ext_send, ext_recv, tile_send, tile_recv, pass_send, pass_recv, out_sem,
):
    r = lax.axis_index("row")
    q = lax.axis_index("pair")
    b = a_ref.shape[1] // 2
    s = b // nr
    first, last = q == 0, q == np_ - 1
    top, low = r == 0, r == nr - 1
    mate = q + 1 - 2 * (q % 2)
    own_p = 2 * r + q % 2

    def remote(src, dst, send, recv, pair, row):
        return pltpu.make_async_remote_copy(
            src_ref=src, dst_ref=dst, send_sem=send, recv_sem=recv,
            device_id={"pair": pair, "row": row}, device_id_type=pl.DeviceIdType.MESH,
        )

    def wait_bytes(ref, sem):
        pltpu.make_async_copy(ref, ref, sem).wait()

    diag = q // 2 == r
    edge = first | last
    away = (q >= 2) & (r == q // 2 - 1)
    tail = last & low
    off = away | ((q == 1) & top) | tail

    barrier = pltpu.get_barrier_semaphore()

    def greet(pair, row):
        pl.semaphore_signal(
            barrier, inc=1, device_id={"pair": pair, "row": row},
            device_id_type=pl.DeviceIdType.MESH,
        )

    def greet_other(pair, row):
        @pl.when(jnp.logical_not((pair == q) & (row == r)))
        def _():
            greet(pair, row)

    for chain in range(2):
        p = q if chain == 0 else own_p
        pa = jnp.maximum(p - 1, 0)
        pb = jnp.minimum(p + 1, np_ - 1)
        greet_other(pa, pa // 2)
        greet_other(pb, pb // 2)
        greet_other(pb, pa // 2)

    def greet_peers(k, carry):
        greet(q, lax.rem(r + k, nr))
        greet(2 * lax.rem(q // 2 + k, nr) + q % 2, r)
        return carry

    lax.fori_loop(1, nr, greet_peers, 0)

    @pl.when(jnp.logical_not(first))
    def _():
        greet(q - 1, r)

    @pl.when(jnp.logical_not(last))
    def _():
        greet(q + 1, r)

    i32 = lambda flag: flag.astype(jnp.int32)
    expected = (
        2 * (nr - 1) + 2 - i32(first) - i32(last)
        + i32(diag) * (4 * nr - 2 * i32(edge))
        + i32(off) * (2 * nr - 2 * i32(tail))
    )
    pl.semaphore_wait(barrier, expected)

    def scatter(chain, row0, col0, p, slot, sem):
        def body(i, carry):
            src = a_ref.at[
                pl.ds(pl.multiple_of(row0 + i * s, s), s), pl.ds(pl.multiple_of(col0, b), b)
            ]
            dr = i if chain == 0 else p // 2
            dq = p if chain == 0 else 2 * i + p % 2
            dst = buf.at[chain, i, slot]
            own = (dr == r) & (dq == q)

            @pl.when(jnp.logical_not(own))
            def _():
                remote(src, dst, sem, first_sem.at[chain], dq, dr).start()

            @pl.when(own)
            def _():
                pltpu.make_async_copy(src, dst, first_sem.at[chain]).start()

            return carry

        lax.fori_loop(0, nr, body, 0)

    for chain in range(2):

        @pl.when(diag)
        def _():
            base = (q % 2) * 2 * b
            f = i32(first)
            scatter(
                chain, base + f * b, (1 - f) * b, jnp.minimum(q + 1, np_ - 1), i32(last),
                sc_sem.at[0],
            )
            scatter(chain, base + (1 - f) * b, f * b, jnp.maximum(q - 1, 0), 1 - f, sc_sem.at[0])

        @pl.when(off)
        def _():
            p = jnp.where(q == 1, 0, jnp.where(tail, np_ - 1, q - 1))
            base = jnp.where(away, q % 2, 0) * 2 * b
            scatter(chain, base, b, p, 2, sc_sem.at[1])
            scatter(chain, base + b, 0, p, 3, sc_sem.at[1])

    def gather(chain):
        me = r if chain == 0 else q // 2
        own = buf.at[chain, me]
        wait_bytes(own, first_sem.at[chain])

        def send(k, carry):
            peer = lax.rem(me + k, nr)
            pair = q if chain == 0 else 2 * peer + q % 2
            row = peer if chain == 0 else r
            remote(own, own, ag_send.at[chain], ag_recv.at[chain], pair, row).start()
            return carry

        lax.fori_loop(1, nr, send, 0)

    gather(0)
    gather(1)
    wait_bytes(buf.at[0, pl.ds(0, nr - 1)], ag_recv.at[0])

    def block(pair, kind):
        at = 2 * pair * b + kind * b
        return a_ref.at[at : at + b, b * (1 - kind) : b * (2 - kind)]

    for side in range(2):
        away_row = low if side == 0 else top
        here_row = top if side == 0 else low
        away_col = last if side == 0 else first
        here_col = first if side == 0 else last
        step = 1 if side == 0 else -1
        for kind in range(2):

            @pl.when(jnp.logical_not(away_row))
            def _():
                remote(
                    block(1 - side, kind), ext.at[side, kind], ext_send.at[side],
                    ext_recv.at[side], q, r + step,
                ).start()

            @pl.when(here_row)
            def _():
                pltpu.make_async_copy(
                    block(side, kind), ext.at[side, kind], ext_recv.at[side]
                ).start()

            for pair in range(2):

                @pl.when(jnp.logical_not(away_col))
                def _():
                    remote(
                        block(pair, kind), tiles.at[side, 1 + pair, kind], tile_send.at[side],
                        tile_recv.at[side], q + step, r,
                    ).start()

                @pl.when(here_col)
                def _():
                    pltpu.make_async_copy(
                        block(pair, kind), tiles.at[side, 1 + pair, kind], tile_recv.at[side]
                    ).start()

    def chain_at(chain, p):
        blocks = [buf[chain, :, k].reshape(b, b) for k in range(4)]
        made = rotations(blocks, p, np_, turns.at[chain], steps_factor({b: 2, 2 * b: 3}))
        for k, value in enumerate(made):
            fits[chain, k] = jnp.full((8, 128), value, F32)

    chain_at(0, q)

    wait_bytes(buf.at[1, pl.ds(0, nr - 1)], ag_recv.at[1])
    spare = remote(buf.at[1], buf.at[2], pass_send.at[0], pass_recv.at[0], mate, r)
    spare.start()
    for side in range(2):
        wait_bytes(ext.at[side], ext_recv.at[side])
    for side in range(2):
        away_col = last if side == 0 else first
        here_col = first if side == 0 else last
        step = 1 if side == 0 else -1
        for k in range(2):

            @pl.when(jnp.logical_not(away_col))
            def _():
                remote(
                    ext.at[k], tiles.at[side, 3 * k], tile_send.at[2 + side],
                    tile_recv.at[2 + side], q + step, r,
                ).start()

            @pl.when(here_col)
            def _():
                pltpu.make_async_copy(
                    ext.at[k], tiles.at[side, 3 * k], tile_recv.at[2 + side]
                ).start()

    chain_at(1, own_p)

    for side in range(2):
        wait_bytes(tiles.at[side, 1:3], tile_recv.at[side])
        wait_bytes(tiles.at[side, 1:3], tile_recv.at[2 + side])
    wait_bytes(buf.at[2], pass_recv.at[0])
    turn = remote(turns.at[1], turns.at[2], pass_send.at[1], pass_recv.at[1], mate, r)
    turn.start()
    fit = remote(fits.at[1], fits.at[2], pass_send.at[2], pass_recv.at[2], mate, r)
    fit.start()
    early = [
        pltpu.make_async_copy(tiles, tiles_out, out_sem.at[0]),
        pltpu.make_async_copy(buf, quads_out, out_sem.at[1]),
        pltpu.make_async_copy(turns.at[0:2], turns_out.at[0:2], out_sem.at[2]),
    ]
    for copy in early:
        copy.start()
    turn.wait_recv()
    late = [pltpu.make_async_copy(turns.at[2], turns_out.at[2], out_sem.at[3])]
    late[0].start()
    fit.wait_recv()
    late.append(pltpu.make_async_copy(fits, fits_out, out_sem.at[4]))
    late[1].start()

    for chain in range(2):
        wait_bytes(buf.at[chain, pl.ds(0, nr - 1)], ag_send.at[chain])
    for side in range(2):

        @pl.when(jnp.logical_not(low if side == 0 else top))
        def _():
            wait_bytes(ext.at[side], ext_send.at[side])

        @pl.when(jnp.logical_not(last if side == 0 else first))
        def _():
            wait_bytes(tiles.at[side, 1:3], tile_send.at[side])
            wait_bytes(ext, tile_send.at[2 + side])

    def drain(pieces, sem):
        wait_bytes(a_ref.at[pl.ds(0, pieces * s), pl.ds(0, b)], sem)

    @pl.when(diag & edge)
    def _():
        drain(4 * nr - 2, sc_sem.at[0])

    @pl.when(diag & jnp.logical_not(edge))
    def _():
        drain(4 * nr, sc_sem.at[0])

    @pl.when(tail)
    def _():
        drain(4 * nr - 4, sc_sem.at[1])

    @pl.when(off & jnp.logical_not(tail))
    def _():
        drain(4 * nr, sc_sem.at[1])

    spare.wait_send()
    turn.wait_send()
    fit.wait_send()
    for copy in early + late:
        copy.wait()


def turned(matrix, nr, np_):
    b = matrix.shape[1] // 2
    quads = (3, nr, 4, b // nr, b)
    turns = (3, 4 * b, 2 * b)
    tiles = (2, 4, 2, b, b)
    fits = (3, 6, 8, 128)
    any_space = pl.BlockSpec(memory_space=pl.ANY)
    dma = pltpu.SemaphoreType.DMA
    return pl.pallas_call(
        functools.partial(turn_kernel, nr, np_),
        out_shape=[
            jax.ShapeDtypeStruct(turns, BF),
            jax.ShapeDtypeStruct(tiles, BF),
            jax.ShapeDtypeStruct(quads, BF),
            jax.ShapeDtypeStruct(fits, F32),
        ],
        in_specs=[any_space],
        out_specs=[any_space] * 4,
        scratch_shapes=[
            pltpu.VMEM(quads, BF),
            pltpu.VMEM(turns, BF),
            pltpu.VMEM(tiles, BF),
            pltpu.VMEM((2, 2, b, b), BF),
            pltpu.VMEM(fits, F32),
            dma((2,)), dma((2,)), dma((2,)), dma((2,)),
            dma((2,)), dma((2,)), dma((4,)), dma((4,)), dma((3,)), dma((3,)), dma((5,)),
        ],
        compiler_params=pltpu.CompilerParams(has_side_effects=True, collective_id=0),
    )(matrix)


def update_kernel(
    np_, fits_ref, tiles_ref, quads_ref, turns_in, out_ref,
    turns, mid, quad, d1, e1, v1, d2, e2, v2, load_sem, quad_sem,
):
    r = lax.axis_index("row")
    q = lax.axis_index("pair")
    core = q % 2
    b = tiles_ref.shape[-1]
    load = pltpu.make_async_copy(turns_in, turns, load_sem)
    load.start()
    load.wait()

    def good(chain):
        value = fits_ref[chain]
        close = [value[k, 0, 0] <= HALT for k in (0, 2, 4)]
        near = [value[k, 0, 0] < WIDE for k in (1, 3, 5)]
        return functools.reduce(jnp.logical_and, close + near)

    def redo(chain, carry):
        @pl.when(jnp.logical_not(good(chain)))
        def _():
            fetch = pltpu.make_async_copy(quads_ref.at[chain], quad, quad_sem)
            fetch.start()
            fetch.wait()
            blocks = [quad[:, k].reshape(b, b) for k in range(4)]
            p = jnp.where(chain == 0, q, jnp.where(chain == 1, 2 * r + core, 2 * r + 1 - core))
            rotations(
                blocks, p, np_, turns.at[chain], full_factor({b: (d1, e1, v1), 2 * b: (d2, e2, v2)})
            )

        return carry

    lax.fori_loop(0, 3, redo, 0)

    for side in range(2):
        cols = slice(side * b, (side + 1) * b)
        even = turns[0, 0:b, cols]
        odd = turns[0, b : 2 * b, cols]
        for k in range(4):
            mid[k, :b, cols] = mm(tiles_ref[side, k, 0], odd).astype(BF)
            mid[k, b:, cols] = mm(tiles_ref[side, k, 1], even).astype(BF)
    turn = turns[0, 2 * b :, :]
    for chain, local in ((1, core), (2, 1 - core)):
        top = mm_tn(turns[chain, : 2 * b, :b], mid[local])
        bottom = mm_tn(turns[chain, : 2 * b, b:], mid[local + 2])
        current = jnp.concatenate([top, bottom], 0).astype(BF)
        columns = mm(current, turn).astype(BF)
        out_ref[pl.ds(pl.multiple_of(local * 2 * b, 2 * b), 2 * b), :] = mm_tn(
            turns[chain, 2 * b :, :], columns
        ).astype(BF)


def updated(turns, tiles, quads, fits, np_):
    b = tiles.shape[-1]
    any_space = pl.BlockSpec(memory_space=pl.ANY)
    vmem = pl.BlockSpec(memory_space=pltpu.VMEM)
    return pl.pallas_call(
        functools.partial(update_kernel, np_),
        out_shape=jax.ShapeDtypeStruct((4 * b, 2 * b), BF),
        in_specs=[vmem, vmem, any_space, any_space],
        out_specs=vmem,
        scratch_shapes=[
            pltpu.VMEM(turns.shape, BF),
            pltpu.VMEM((4, 2 * b, 2 * b), BF),
            pltpu.VMEM(quads.shape[1:], BF),
        ]
        + [pltpu.VMEM((b, b), F32)] * 3
        + [pltpu.VMEM((2 * b, 2 * b), F32)] * 3
        + [pltpu.SemaphoreType.DMA, pltpu.SemaphoreType.DMA],
    )(fits, tiles, quads, turns)


def local(matrix):
    nr = lax.axis_size("row")
    np_ = lax.axis_size("pair")
    turns, tiles, quads, fits = turned(matrix, nr, np_)
    return updated(turns, tiles, quads, fits, np_)


def solution(mesh):
    return jax.shard_map(
        local, mesh=mesh, in_specs=(P("row", "pair"),), out_specs=P("row", "pair"), check_vma=False
    )
```

time: 803 us -> 128 us (0.16)
  the two profiles are of different devices: /device:TPU:1 before, /device:TPU:134 now
where the time goes in v2:
time: 128 us; the launch traced here: 127 us
  Pallas kernels  127 us (99%)
    pallas_call x1, Pallas kernels, turned(): pl.pallas_call(functools.partial(turn_kernel, nr, np_), out_shape=[jax.Sh...  75.8 us
    pallas_call x1, Pallas kernels, updated(): pl.pallas_call(functools.partial(update_kernel, np_), out_shape=jax.Shape...  51.2 us

profile of v2, /device:TPU:134, one launch (start us, length us, event | category | flops | bytes accessed | tf_op | source)
XLA Modules:
  0.0 127.2 jit_solution(18039159342962307385)
XLA Ops:
  0.0 75.8 %shard_map.17 = (bf16[3,1024,512]{2,1,0:T(8,128)(2,1)}, bf16[2,4,2,256,256]{4,3,2,1,0:T(8,128)(2,1)}, bf16[3,16,4,16,256]{4,3,2,1,0:T(8,128)(2,1)}, f32[3,6,8,128]{3,2,1,0:T(8,128)}) custom-call(bf16[1024,512]{1,0:T(8,128)(2,1)} %a_ref.1), custom_call_target="tpu_custom_call" | custom-call | tf_op jit(solution)/shard_map/pallas_call | solution.py:467
  75.8 51.2 %shard_map.18 = bf16[1024,512]{1,0:T(8,128)(2,1)} custom-call(f32[3,6,8,128]{3,2,1,0:T(8,128)} %get-tuple-element.9.fits_ref, bf16[2,4,2,256,256]{4,3,2,1,0:T(8,128)(2,1)} %get-tuple-element.10.tiles_ref, bf16[3,16,4,16,256]{4,3,2,1,0:T(8,128)(2,1)} %get-tuple-element.11.quads_ref, bf16[3,1024,512]{2,1,0:T(8,128)(2,1)} %get-tuple-element.12.turns_in), custom_call_target="tpu_custom_call" | custom-call | tf_op jit(solution)/shard_map/pallas_call | solution.py:546
